TPU v7x, 32 devices: a whole 2x2x4 slice. The times are simulated.
32 devices in a mesh: grp: 2 (over y), var: 8 (over z, x), smp: 2 (over core).
Axes of the slice: x: 2, y: 2, z: 4, core: 2. Of those that a mesh axis runs over, the one named last changes fastest.
Arguments:
- genotypes: bfloat16 [15360, 1024], P(('grp', 'smp'), 'var'), parts along dimension 0, may hold values from 0 to 2, as said below
- ancestry_counts: int32 [15360, 32], P(('grp', 'smp')), parts along dimension 0, may hold values from 1 to 100
- residuals: int32 [15360, 16], P(('grp', 'smp')), parts along dimension 0, may hold values from -3000 to 3000
- freqs: float32 [64, 1024], P('grp', 'var'), parts along dimension 0, may hold values from 0.05 to 0.95
Outputs:
- q_new: float32 [15360, 32], P(('grp', 'smp', 'var')), parts along dimension 0
- q_gradient: float32 [15360, 32], P(('grp', 'smp', 'var')), parts along dimension 0
- p_new: float32 [64, 1024], P('grp', 'var'), parts along dimension 0
- p_gradient: float32 [64, 1024], P('grp', 'var'), parts along dimension 0
- z_score: float32 [64, 16, 1024], P('grp', None, 'var'), parts along dimension 0
There are 2 independent parts, one for each index of `grp`. A program takes and returns all parts, laid end to end along the dimension named above; each array names one. Nothing has to cross between parts.
Inputs may be any that keep to these rules, and one draw needn't show every extreme that they name: `genotypes`: dosages lie in the closed range from 0 to 2.
All inputs are finite; a program needn't handle non-finite values.
Results may differ from a plain program's by a relative error of at most 0.0003.
Values sent between devices are 32-bit elements; how exact they have to be, the bound alone decides.
A program may use at most 64 MiB of HBM per device.

v0:
```python
import math

import jax
import jax.numpy as jnp
from jax import lax
from jax.sharding import PartitionSpec as P


def normalize(fractions, gradient, second):
    weighted = fractions * (gradient + second[:, None])
    return weighted / jnp.sum(weighted, axis=1, keepdims=True)


def update_freqs(freqs, excess_sum, second_sum, sample_count):
    allele_sum = excess_sum + second_sum
    freq_next = freqs * allele_sum / (freqs * allele_sum + (1.0 - freqs) * second_sum)
    freq_gradient = excess_sum * freqs.shape[0] / math.sqrt(sample_count)
    return (freq_next, freq_gradient)


def shards(genotypes, ancestry_counts, residuals, freqs):
    highest = lax.Precision.HIGHEST
    var_count = lax.axis_size("var")
    sample_rows = genotypes.shape[0]
    sample_count = sample_rows * lax.axis_size("smp")
    variant_count = genotypes.shape[1] * var_count
    anc_count = freqs.shape[0]
    trait_count = residuals.shape[1]
    counts = ancestry_counts.astype(jnp.float32)
    fractions = counts / jnp.sum(counts, axis=1, keepdims=True)
    dosage = genotypes.astype(jnp.float32)
    recon_rows = jnp.dot(fractions, freqs, precision=highest)
    ratio_a = dosage / recon_rows
    ratio_b = (2.0 - dosage) / (1.0 - recon_rows)
    excess = ratio_a - ratio_b
    gradient_part = jnp.dot(excess, freqs.T, precision=highest)
    second_part = jnp.sum(ratio_b, axis=1)
    excess_part = jnp.dot(fractions.T, excess, precision=highest)
    return_part = jnp.dot(fractions.T, ratio_b, precision=highest)
    share_rows = sample_rows // var_count
    first_row = lax.axis_index("var") * share_rows
    excess_sum, second_sum = lax.psum((excess_part, return_part), "smp")
    freq_next, freq_gradient = update_freqs(freqs, excess_sum, second_sum, sample_count)
    gradient_all, second_all = lax.psum((gradient_part, second_part), "var")
    fraction_next = normalize(fractions, gradient_all, second_all)
    own_next = lax.dynamic_slice_in_dim(fraction_next, first_row, share_rows, 0)
    own_gradient = lax.dynamic_slice_in_dim(gradient_all, first_row, share_rows, 0)
    scaled_gradient = own_gradient / math.sqrt(variant_count)
    ratio_next = dosage / jnp.dot(fraction_next, freqs, precision=highest)
    residual = residuals.astype(jnp.float32) / 1000.0
    trait_rows = (fraction_next[:, :, None] * residual[:, None, :]).reshape(
        sample_rows, anc_count * trait_count
    )
    score_part = jnp.dot(trait_rows.T, ratio_next, precision=highest)
    info_part = jnp.dot(
        (fraction_next * fraction_next).T, ratio_next * ratio_next, precision=highest
    )
    score_sum, info_sum = lax.psum((score_part, info_part), "smp")
    score_tiles = score_sum.reshape(anc_count, trait_count, genotypes.shape[1])
    z_score = score_tiles / jnp.sqrt(info_sum + 1e-06)[:, None, :]
    return (own_next, scaled_gradient, freq_next, freq_gradient, z_score)


def solution(mesh):
    in_specs = (
        P(("grp", "smp"), "var"),
        P(("grp", "smp"), None),
        P(("grp", "smp"), None),
        P("grp", "var"),
    )
    out_specs = (
        P(("grp", "smp", "var"), None),
        P(("grp", "smp", "var"), None),
        P("grp", "var"),
        P("grp", "var"),
        P("grp", None, "var"),
    )
    return jax.shard_map(shards, mesh=mesh, in_specs=in_specs, out_specs=out_specs, check_vma=False)
```

profile of v0, /device:TPU:0, one launch (start us, length us, event | category | flops | bytes accessed | tf_op | source)
XLA Modules:
  0.0 131.7 jit_solution(6251124722498044201)
XLA Ops:
  7.2 0.0 copy-start
  7.2 0.0 copy-start.2
  7.2 0.0 all-reduce.4.cloned.1.call-start
  7.2 1.1 convert_reduce_fusion
  8.4 1.6 %copy.13 = bf16[3840,128]{0,1:T(8,128)(2,1)S(1)} copy(bf16[3840,128]{1,0:T(8,128)(2,1)} %param.4) | data formatting | bytes 1966080 | tf_op args[0]
  9.9 0.0 copy-done
  9.9 0.0 copy-done.2
  10.0 3.5 %fusion.8 = (f32[3840]{0:T(1024)S(1)}, f32[3840,128]{0,1:T(8,128)S(1)}, f32[3840,128]{0,1:T(8,128)}) fusion(bf16[3840,128]{0,1:T(8,128)(2,1)S(1)} %copy.13, f32[32,128]{1,0:T(8,128)S(1)} %copy-done.2, s32[3840,32]{0,1:T(8,128)S(1)} %copy-done, f32[3840]{0:T(1024)S(1)} %convert_reduce_fusion), kind=kOutput, calls=%fused_computation.22 | convolution fusion | flops 192426240 | bytes 5453824 | tf_op jit(solution)/shard_map/dot_general | solution.py:32
  13.5 2.0 %fusion.11 = f32[3840,32]{0,1:T(8,128)} fusion(f32[3840,128]{0,1:T(8,128)S(1)} %get-tuple-element.9, f32[32,128]{1,0:T(8,128)S(1)} %copy-done.2), kind=kOutput, calls=%fused_computation.25 | convolution fusion | flops 188743680 | bytes 2473984 | tf_op jit(solution)/shard_map/dot_general | solution.py:36
  15.4 0.0 all-reduce.4.cloned.1.call-update
  15.5 0.0 all-reduce.6.cloned.1.call-start
  15.5 1.7 %convert_multiply_fusion = f32[3840,16]{0,1:T(8,128)} fusion(s32[3840,16]{0,1:T(8,128)} %param.6), kind=kLoop, calls=%fused_computation.12 | loop fusion | flops 122880 | bytes 491520 | tf_op jit(solution)/shard_map/div | solution.py:50
  17.2 2.0 %fusion.9 = f32[32,128]{1,0:T(8,128)S(1)} fusion(f32[3840,128]{0,1:T(8,128)S(1)} %get-tuple-element.9, s32[3840,32]{0,1:T(8,128)S(1)} %copy-done, f32[3840]{0:T(1024)S(1)} %convert_reduce_fusion), kind=kOutput, calls=%fused_computation.23 | convolution fusion | flops 188989440 | bytes 2489344 | tf_op jit(solution)/shard_map/dot_general | solution.py:38
  19.2 38.9 %psum.43 = f32[3840]{0:T(1024)S(1)} all-reduce(f32[3840]{0:T(1024)S(1)} %get-tuple-element.8), channel_id=1, replica_groups=mesh['grp'=2,'var'=8,'smp'=2] {'var'}, use_global_device_ids=true, to_apply=%region_3.0 | all-reduce | flops 3840 | bytes 30720 | tf_op jit(solution)/shard_map/psum | solution.py:44
  58.0 3.5 %fusion.6 = f32[32,128]{1,0:T(8,128)S(1)} fusion(bf16[3840,128]{0,1:T(8,128)(2,1)S(1)} %copy.13, f32[3840,128]{0,1:T(8,128)} %get-tuple-element.12, s32[3840,32]{0,1:T(8,128)S(1)} %copy-done, f32[3840]{0:T(1024)S(1)} %convert_reduce_fusion), kind=kOutput, calls=%fused_computation.21 | convolution fusion | flops 190955520 | bytes 3472384 | tf_op jit(solution)/shard_map/dot_general | solution.py:39
  61.6 29.5 %all-reduce.4.cloned.1.call-done = f32[3840,32]{0,1:T(8,128)} async-done(((f32[3840,32]{0,1:T(8,128)}), f32[3840,32]{0,1:T(8,128)}) %all-reduce.4.cloned.1.call-update) | async-done | bytes 491536 | tf_op jit(solution)/shard_map/psum | solution.py:44
  91.1 1.1 fusion.5
  92.3 1.1 broadcast_divide_fusion
  93.4 1.8 %convolution_divide_fusion = f32[3840,128]{0,1:T(8,128)S(1)} fusion(f32[3840,32]{0,1:T(8,128)S(1)} %broadcast_divide_fusion, f32[32,128]{1,0:T(8,128)S(1)} %copy-done.2, bf16[3840,128]{0,1:T(8,128)(2,1)S(1)} %copy.13), kind=kOutput, calls=%fused_computation | convolution fusion | flops 189726720 | bytes 3457024 | tf_op jit(solution)/shard_map/dot_general | solution.py:49
  95.2 0.0 copy-start.1
  95.2 0.7 constant_dynamic-slice_fusion
  95.9 2.0 %fusion.2 = f32[32,128]{1,0:T(8,128)S(1)} fusion(f32[3840,128]{0,1:T(8,128)S(1)} %convolution_divide_fusion, f32[3840,32]{0,1:T(8,128)S(1)} %broadcast_divide_fusion), kind=kOutput, calls=%fused_computation.6 | convolution fusion | flops 189358080 | bytes 2473984 | tf_op jit(solution)/shard_map/dot_general | solution.py:55
  97.9 0.0 copy-done.1
  98.0 0.9 broadcast_multiply_fusion
  98.8 6.9 %fusion.12 = f32[512,128]{1,0:T(8,128)} fusion(f32[3840,512]{0,1:T(8,128)S(1)} %bitcast.10, f32[3840,128]{0,1:T(8,128)S(1)} %convolution_divide_fusion), kind=kOutput, calls=%fused_computation.26 | convolution fusion | flops 3019898880 | bytes 10092544 | tf_op jit(solution)/shard_map/dot_general | solution.py:54
  105.8 0.0 all-reduce.6.cloned.1.call-update
  105.8 1.6 %dynamic-slice_multiply_fusion = f32[480,32]{0,1:T(8,128)} fusion(f32[3840,32]{0,1:T(8,128)} %all-reduce.4.cloned.1.call-done, s32[]{:T(128)S(6)} %select_n.4), kind=kLoop, calls=%fused_computation.16 | loop fusion | flops 15360 | bytes 122884 | tf_op jit(solution)/shard_map/div | solution.py:48
  107.4 3.5 %all-reduce = (f32[32,128]{1,0:T(8,128)S(1)}, f32[32,128]{1,0:T(8,128)S(1)}, f32[32,128]{1,0:T(8,128)S(1)}) all-reduce(f32[32,128]{1,0:T(8,128)S(1)} %fusion.6, f32[32,128]{1,0:T(8,128)S(1)} %fusion.9, f32[32,128]{1,0:T(8,128)S(1)} %fusion.2), channel_id=1, replica_groups=mesh['grp'=2,'var'=8,'smp'=2] {'smp'}, use_global_device_ids=true, to_apply=%region_6.0 | all-reduce | flops 12288 | bytes 98304 | tf_op jit(solution)/shard_map/psum | solution.py:42
  111.0 0.6 broadcast_multiply_fusion.1
  111.6 11.6 %all-reduce.6.cloned.1.call-done = f32[32,16,128]{2,1,0:T(8,128)} async-done(((f32[32,16,128]{2,1,0:T(8,128)}), f32[32,16,128]{2,1,0:T(8,128)}) %all-reduce.6.cloned.1.call-update) | async-done | bytes 262160 | tf_op jit(solution)/shard_map/psum | solution.py:58
  123.2 1.7 %broadcast_divide_fusion.1 = f32[32,16,128]{2,1,0:T(8,128)} fusion(f32[32,16,128]{2,1,0:T(8,128)} %all-reduce.6.cloned.1.call-done, f32[32,128]{1,0:T(8,128)S(1)} %get-tuple-element.13), kind=kLoop, calls=%fused_computation.15 | loop fusion | flops 65536 | bytes 540672 | tf_op jit(solution)/shard_map/div | solution.py:60
Async XLA Ops:
  7.2 2.8 %copy-start = (s32[3840,32]{0,1:T(8,128)S(1)}, s32[3840,32]{0,1:T(8,128)}, u32[]{:S(2)}) copy-start(s32[3840,32]{0,1:T(8,128)} %param.5) | copy-start | bytes 1474564
  7.2 2.8 %copy-start.2 = (f32[32,128]{1,0:T(8,128)S(1)}, f32[32,128]{1,0:T(8,128)}, u32[]{:S(2)}) copy-start(f32[32,128]{1,0:T(8,128)} %param.7) | copy-start | bytes 49156
  7.2 83.9 %all-reduce.4.cloned.1.call-start = ((), (), s32[]{:S(2)}) async-start(), calls=%async_computation | async-start | bytes 983040 | tf_op jit(solution)/shard_map/psum | solution.py:44
  15.5 107.7 %all-reduce.6.cloned.1.call-start = ((), (), s32[]{:S(2)}) async-start(), calls=%async_computation.1 | async-start | bytes 524288 | tf_op jit(solution)/shard_map/psum | solution.py:58
  95.2 2.8 %copy-start.1 = (f32[3840,16]{0,1:T(8,128)S(1)}, f32[3840,16]{0,1:T(8,128)}, u32[]{:S(2)}) copy-start(f32[3840,16]{0,1:T(8,128)} %convert_multiply_fusion) | copy-start | bytes 737284
Sparse Core Ops, SparseCore 0:
  15.6 75.4 all-reduce.3
  105.9 17.2 all-reduce.5
where the time goes:
time: 132 us
  blocking collectives  42.4 us (32%)
  waiting for transfers between devices  41.2 us (31%)
  matrix products  21.7 us (16%)
  between operations  14.2 us (11%)
  other arithmetic  9.86 us (7%)
  local copies, waits for them, and re-layouts  2.3 us (2%)
    psum x1, blocking collectives, shards(): gradient_all, second_all = lax.psum((gradient_part, second_part), 'var')  38.9 us
    psum x1, waiting for transfers between devices, shards(): gradient_all, second_all = lax.psum((gradient_part, second_part), 'var')  29.5 us
    psum x1, waiting for transfers between devices, shards(): score_sum, info_sum = lax.psum((score_part, info_part), 'smp')  11.6 us
    dot_general x1, matrix products, shards(): score_part = jnp.dot(trait_rows.T, ratio_next, precision=highest)  6.95 us
    psum x1, blocking collectives, shards(): excess_sum, second_sum = lax.psum((excess_part, return_part), 'smp')  3.54 us
    dot_general x1, matrix products, shards(): return_part = jnp.dot(fractions.T, ratio_b, precision=highest)  3.53 us
    dot_general x1, matrix products, shards(): recon_rows = jnp.dot(fractions, freqs, precision=highest)  3.49 us
  transfers between devices with their start and end apart: 2, of which 2 were waited for; matrix products, arithmetic and copies ran while one was open for 7% of the time, Pallas kernels for 0%

commit v1 on v0

--- a/solution.py
+++ b/solution.py
@@ -1,9 +1,16 @@
+import functools
 import math
 
 import jax
 import jax.numpy as jnp
 from jax import lax
+from jax.experimental import pallas as pl
+from jax.experimental.pallas import tpu as pltpu
 from jax.sharding import PartitionSpec as P
+
+MESH = pl.DeviceIdType.MESH
+F32 = jnp.float32
+BF16 = jnp.bfloat16
 
 
 def normalize(fractions, gradient, second):
@@ -18,7 +25,7 @@
     return (freq_next, freq_gradient)
 
 
-def shards(genotypes, ancestry_counts, residuals, freqs):
+def shards_plain(genotypes, ancestry_counts, residuals, freqs):
     highest = lax.Precision.HIGHEST
     var_count = lax.axis_size("var")
     sample_rows = genotypes.shape[0]
@@ -61,6 +68,304 @@
     return (own_next, scaled_gradient, freq_next, freq_gradient, z_score)
 
 
+def split(x):
+    high = x.astype(BF16)
+    return high, (x - high.astype(F32)).astype(BF16)
+
+
+def dot(a, b):
+    return jnp.dot(a, b, preferred_element_type=F32)
+
+
+def dot_lanes(a, b):
+    return lax.dot_general(a, b, (((1,), (1,)), ((), ())), preferred_element_type=F32)
+
+
+def kernel(
+    dims,
+    geno, counts, resid, freqs,
+    q_out, g_out, p_out, pg_out, z_out,
+    dos, qf, gf, fcol, frow, ebuf, tbuf,
+    acc_ex, acc_sc, acc_in,
+    xs, xr, zs, zr, go, gp, fs, fr, ss, sr,
+    xs_s, xs_r, zs_s, zs_r, za_s, za_r, xa_s, xa_r, f_s, f_r, s_s, s_r,
+):
+    chunks, width, half, zs_n, rows, variant_count, sample_count, share, var_n = dims
+    anc = freqs.shape[0]
+    traits = resid.shape[0]
+    mv = freqs.shape[1]
+    me = lax.axis_index("var")
+    core = lax.axis_index("smp")
+    x = lax.rem(me, 2)
+    z = me // 2
+    partner = {"var": z * 2 + (1 - x)}
+    twin = {"smp": 1 - core}
+    z_peers = [{"var": lax.rem(z + d, zs_n) * 2 + x} for d in range(1, zs_n)]
+
+    barrier = pltpu.get_barrier_semaphore()
+    for peer in [partner, twin] + z_peers:
+        pl.semaphore_signal(barrier, inc=1, device_id=peer, device_id_type=MESH)
+
+    p = freqs[...]
+    p_hi, p_lo = split(p)
+    stack = jnp.concatenate([p_hi.astype(F32), p_lo.astype(F32)] * 2, axis=0)
+    fcol[...] = stack.T.astype(BF16)
+    frow[0:anc, 0:mv] = p_hi
+    frow[0:anc, mv:] = p_hi
+    frow[anc:, 0:mv] = p_lo
+    frow[anc:, mv:] = p_lo
+    acc_ex[...] = jnp.zeros_like(acc_ex)
+    acc_sc[...] = jnp.zeros_like(acc_sc)
+    acc_in[...] = jnp.zeros_like(acc_in)
+
+    def lanes(which, c):
+        return pl.multiple_of(which * half + c * width, 128)
+
+    def first_pass(off):
+        d = geno[pl.ds(off, width), :].astype(F32).T
+        dos[:, pl.ds(off, width)] = d.astype(BF16)
+        c = counts[:, pl.ds(off, width)].astype(F32)
+        total = jnp.sum(c, axis=0, keepdims=True)
+        cb = c.astype(BF16)
+        none = jnp.zeros_like(cb)
+        u = dot(fcol[...], jnp.concatenate([cb, cb, none, none], axis=0))
+        w = total - u
+        inverse = 1.0 / (u * w)
+        b = (2.0 - d) * u * inverse
+        e = d * w * inverse - b
+        e_hi, e_lo = split(e)
+        b_hi, b_lo = split(b)
+        ebuf[0:mv, :] = e_hi
+        ebuf[mv : 2 * mv, :] = e_lo
+        ebuf[2 * mv : 3 * mv, :] = b_hi
+        ebuf[3 * mv :, :] = b_lo
+        g = dot(frow[...], ebuf[0 : 2 * mv, :])
+        acc_ex[...] += dot_lanes(ebuf[...], jnp.concatenate([cb] * (128 // anc), axis=0))
+        return (g[0:anc, :] + g[anc:, :]) * total
+
+    def second_pass(off, g):
+        c = counts[:, pl.ds(off, width)].astype(F32)
+        f = c / jnp.sum(c, axis=0, keepdims=True)
+        second = 2.0 * variant_count - jnp.sum(f * g, axis=0, keepdims=True)
+        weighted = f * (g + second)
+        q = weighted / jnp.sum(weighted, axis=0, keepdims=True)
+        qf[:, pl.ds(off, width)] = q
+        gf[:, pl.ds(off, width)] = g * (1.0 / math.sqrt(variant_count))
+        q_hi, q_lo = split(q)
+        recon = dot(fcol[...], jnp.concatenate([q_hi, q_hi, q_lo, q_lo], axis=0))
+        r = dos[:, pl.ds(off, width)].astype(F32) / recon
+        r_hi, r_lo = split(r)
+        s_hi, s_lo = split(r * r)
+        t = resid[:, pl.ds(off, width)].astype(F32)
+        for k in range(anc):
+            t_hi, t_lo = split(q[k : k + 1, :] * t)
+            tbuf[traits * k : traits * (k + 1), 0:width] = t_hi
+            tbuf[traits * k : traits * (k + 1), width:] = t_lo
+        r_cat = jnp.concatenate([r_hi, r_lo], axis=0)
+        acc_sc[...] += dot_lanes(tbuf[...], jnp.concatenate([r_cat, r_cat], axis=1))
+        y_hi, y_lo = split(q * q)
+        none = jnp.zeros_like(y_hi)
+        acc_in[...] += dot_lanes(
+            jnp.concatenate([s_hi, s_lo], axis=0),
+            jnp.concatenate([y_hi, y_lo, none, none], axis=0),
+        )
+
+    def copy(src, dst, send, recv, peer):
+        return pltpu.make_async_remote_copy(
+            src_ref=src, dst_ref=dst, send_sem=send, recv_sem=recv, device_id=peer, device_id_type=MESH
+        )
+
+    def x_reduce(c):
+        return copy(xs.at[c], xr.at[c], xs_s.at[c], xs_r.at[c], partner)
+
+    def z_reduce(c, d):
+        to = pl.multiple_of(lax.rem(z + d, zs_n) * rows, 8)
+        return copy(
+            zs.at[c, pl.ds(to, rows), :], zr.at[c, d - 1], zs_s.at[c, d - 1], zs_r.at[c, d - 1], z_peers[d - 1]
+        )
+
+    mine = pl.multiple_of(z * rows, 8)
+
+    def z_gather(c, d):
+        piece = go.at[c, pl.ds(mine, rows), :]
+        return copy(piece, piece, za_s.at[c, d - 1], za_r.at[c, d - 1], z_peers[d - 1])
+
+    def z_gathered(c, d):
+        source = pl.multiple_of(lax.rem(z + zs_n - d, zs_n) * rows, 8)
+        piece = go.at[c, pl.ds(source, rows), :]
+        return copy(piece, piece, za_s.at[c, d - 1], za_r.at[c, d - 1], z_peers[d - 1])
+
+    def x_gather(c):
+        return copy(go.at[c], gp.at[c], xa_s.at[c], xa_r.at[c], partner)
+
+    pl.semaphore_wait(barrier, 2 + len(z_peers))
+
+    def step_far(c, carry):
+        xs[c] = first_pass(lanes(1 - x, c))
+        x_reduce(c).start()
+        return carry
+
+    lax.fori_loop(0, chunks, step_far, 0)
+
+    def step_near(c, carry):
+        g = first_pass(lanes(x, c))
+        x_reduce(c).wait_recv()
+        zs[c] = g + xr[c]
+        for d in range(1, zs_n):
+            z_reduce(c, d).start()
+        return carry
+
+    lax.fori_loop(0, chunks, step_near, 0)
+
+    ex = acc_ex[0:mv, :] + acc_ex[mv : 2 * mv, :]
+    re = acc_ex[2 * mv : 3 * mv, :] + acc_ex[3 * mv :, :]
+    fs[0:anc, :] = ex.T[0:anc, :]
+    fs[anc:, :] = re.T[0:anc, :]
+    freq_copy = copy(fs, fr, f_s, f_r, twin)
+    freq_copy.start()
+
+    def step_sum(c, carry):
+        total = zs[c, pl.ds(mine, rows), :]
+        for d in range(1, zs_n):
+            z_reduce(c, d).wait_recv()
+            total = total + zr[c, d - 1]
+        go[c, pl.ds(mine, rows), :] = total
+        for d in range(1, zs_n):
+            z_gather(c, d).start()
+        return carry
+
+    lax.fori_loop(0, chunks, step_sum, 0)
+
+    freq_copy.wait_recv()
+    sums = fs[...] + fr[...]
+    excess_sum = sums[0:anc, :]
+    second_sum = sums[anc:, :]
+    freq_next, freq_gradient = update_freqs(p, excess_sum, second_sum, sample_count)
+    p_out[...] = freq_next
+    pg_out[...] = freq_gradient
+
+    def step_own(c, carry):
+        for d in range(1, zs_n):
+            z_gathered(c, d).wait_recv()
+        x_gather(c).start()
+        second_pass(lanes(x, c), go[c])
+        return carry
+
+    lax.fori_loop(0, chunks, step_own, 0)
+
+    def step_other(c, carry):
+        x_gather(c).wait_recv()
+        second_pass(lanes(1 - x, c), gp[c])
+        return carry
+
+    lax.fori_loop(0, chunks, step_other, 0)
+
+    tiles = anc * traits
+    ss[0:tiles, :] = acc_sc[:, 0:mv] + acc_sc[:, mv:]
+    info = (acc_in[0:mv, :] + acc_in[mv:, :]).T
+    ss[tiles:, :] = info[0:anc, :] + info[anc : 2 * anc, :]
+    score_copy = copy(ss, sr, s_s, s_r, twin)
+    score_copy.start()
+
+    for v in range(var_n):
+
+        @pl.when(me == v)
+        def _():
+            q_out[...] = qf[:, share * v : share * (v + 1)]
+            g_out[...] = gf[:, share * v : share * (v + 1)]
+
+    def drain(c, carry):
+        x_reduce(c).wait_send()
+        x_gather(c).wait_send()
+        for d in range(1, zs_n):
+            z_reduce(c, d).wait_send()
+            z_gather(c, d).wait_send()
+        return carry
+
+    lax.fori_loop(0, chunks, drain, 0)
+    freq_copy.wait_send()
+    score_copy.wait_recv()
+    info_sum = ss[tiles:, :] + sr[tiles:, :]
+    scale = 0.001 / jnp.sqrt(info_sum + 1e-06)
+    for k in range(anc):
+        at = slice(traits * k, traits * (k + 1))
+        z_out[at, :] = (ss[at, :] + sr[at, :]) * scale[k : k + 1, :]
+    score_copy.wait_send()
+
+
+def fits(genotypes, residuals, freqs, var_n):
+    samples, mv = genotypes.shape
+    anc = freqs.shape[0]
+    return (
+        var_n == 8
+        and lax.axis_size("smp") == 2
+        and anc == 32
+        and mv == 128
+        and residuals.shape[1] % 16 == 0
+        and samples % (2 * 128) == 0
+        and samples % var_n == 0
+    )
+
+
+def shards(genotypes, ancestry_counts, residuals, freqs):
+    var_n = lax.axis_size("var")
+    if not fits(genotypes, residuals, freqs, var_n):
+        return shards_plain(genotypes, ancestry_counts, residuals, freqs)
+    samples, mv = genotypes.shape
+    anc = freqs.shape[0]
+    traits = residuals.shape[1]
+    zs_n = var_n // 2
+    rows = anc // zs_n
+    half = samples // 2
+    tiles = half // 128
+    chunks = max(n for n in range(1, 6) if tiles % n == 0)
+    width = half // chunks
+    share = samples // var_n
+    dims = (chunks, width, half, zs_n, rows, mv * var_n, samples * lax.axis_size("smp"), share, var_n)
+    vmem = pl.BlockSpec(memory_space=pltpu.VMEM)
+    dma = pltpu.SemaphoreType.DMA
+    part = pltpu.VMEM((chunks, anc, width), F32)
+    q_t, g_t, p_new, p_grad, z_flat = pl.pallas_call(
+        functools.partial(kernel, dims),
+        out_shape=(
+            jax.ShapeDtypeStruct((anc, share), F32),
+            jax.ShapeDtypeStruct((anc, share), F32),
+            jax.ShapeDtypeStruct((anc, mv), F32),
+            jax.ShapeDtypeStruct((anc, mv), F32),
+            jax.ShapeDtypeStruct((anc * traits, mv), F32),
+        ),
+        in_specs=[vmem] * 4,
+        out_specs=(vmem,) * 5,
+        scratch_shapes=[
+            pltpu.VMEM((mv, samples), BF16),
+            pltpu.VMEM((anc, samples), F32),
+            pltpu.VMEM((anc, samples), F32),
+            pltpu.VMEM((mv, 4 * anc), BF16),
+            pltpu.VMEM((2 * anc, 2 * mv), BF16),
+            pltpu.VMEM((4 * mv, width), BF16),
+            pltpu.VMEM((anc * traits, 2 * width), BF16),
+            pltpu.VMEM((4 * mv, 128), F32),
+            pltpu.VMEM((anc * traits, 2 * mv), F32),
+            pltpu.VMEM((2 * mv, 128), F32),
+            part, part, part,
+            pltpu.VMEM((chunks, zs_n - 1, rows, width), F32),
+            part, part,
+            pltpu.VMEM((2 * anc, mv), F32),
+            pltpu.VMEM((2 * anc, mv), F32),
+            pltpu.VMEM((anc * traits + anc, mv), F32),
+            pltpu.VMEM((anc * traits + anc, mv), F32),
+            dma((chunks,)), dma((chunks,)),
+            dma((chunks, zs_n - 1)), dma((chunks, zs_n - 1)),
+            dma((chunks, zs_n - 1)), dma((chunks, zs_n - 1)),
+            dma((chunks,)), dma((chunks,)),
+            dma, dma, dma, dma,
+        ],
+        compiler_params=pltpu.CompilerParams(collective_id=0, has_side_effects=True),
+        name="em_step",
+    )(genotypes, ancestry_counts.T, residuals.T, freqs)
+    return (q_t.T, g_t.T, p_new, p_grad, z_flat.reshape(anc, traits, mv))
+
+
 def solution(mesh):
     in_specs = (
         P(("grp", "smp"), "var"),

time: 132 us -> 37.4 us (0.28)
  blocking collectives: 42.4 us -> 0 us
  waiting for transfers between devices: 41.2 us -> 0 us
  Pallas kernels: 0 us -> 30.8 us
  matrix products: 21.7 us -> 0 us
  between operations: 14.2 us -> 0.65 us
  other arithmetic: 9.86 us -> 0 us
  local copies, waits for them, and re-layouts: 2.3 us -> 5.64 us
    psum x2 -> x0, blocking collectives: 42.4 us -> none  [the longest x1 38.9 us: shards(): gradient_all, second_all = lax.psum((gradient_part, second_part), 'var')]
    psum x2 -> x0, waiting for transfers between devices: 41.1 us -> none  [the longest x1 29.5 us: shards(): gradient_all, second_all = lax.psum((gradient_part, second_part), 'var')]
    pallas_call x0 -> x1, Pallas kernels: none -> 30.8 us  [shards(): pl.pallas_call(functools.partial(kernel, dims), out_shape=(jax.ShapeDtype...]
    dot_general x7 -> x0, matrix products: 21.7 us -> none  [the longest x1 6.95 us: shards(): score_part = jnp.dot(trait_rows.T, ratio_next, precision=highest)]
    div x5 -> x0, other arithmetic: 6.7 us -> none  [the longest x1 1.68 us: shards(): z_score = score_tiles / jnp.sqrt(info_sum + 1e-06)[:, None, :]]
    unnamed x7 -> x9, local copies, waits for them, and re-layouts: 1.57 us -> 5.64 us
    reduce_sum x2 -> x0, other arithmetic: 2.28 us -> none  [the longest x1 1.15 us: normalize(): return weighted / jnp.sum(weighted, axis=1, keepdims=True)]
  transfers between devices with their start and end apart: 2 -> 0, of which waited for: 2 -> 0; matrix products, arithmetic and copies ran while one was open for 7% -> 0% of each run, Pallas kernels for 0% -> 0%
where the time goes in v1:
time: 37.4 us; the launch traced here: 37.1 us
  Pallas kernels  30.8 us (82%)
  local copies, waits for them, and re-layouts  5.64 us (15%)
  between operations  0.65 us (2%)
    pallas_call x1, Pallas kernels, shards(): pl.pallas_call(functools.partial(kernel, dims), out_shape=(jax.ShapeDtype...  30.8 us
    unnamed x9, local copies, waits for them, and re-layouts  5.64 us

profile of v1, /device:TPU:0, one launch (start us, length us, event | category | flops | bytes accessed | tf_op | source)
XLA Modules:
  0.0 37.1 jit_solution(13161238342689095519)
XLA Ops:
  0.6 30.8 %em_step.1 = (f32[32,480]{1,0:T(8,128)}, f32[32,480]{1,0:T(8,128)}, f32[32,128]{1,0:T(8,128)}, f32[32,128]{1,0:T(8,128)}, f32[512,128]{1,0:T(8,128)}) custom-call(bf16[3840,128]{1,0:T(8,128)(2,1)} %geno.1, s32[32,3840]{1,0:T(8,128)} %bitcast.5, s32[16,3840]{1,0:T(8,128)} %bitcast.7, f32[32,128]{1,0:T(8,128)} %freqs.1), custom_call_target="tpu_custom_call" | custom-call | tf_op jit(solution)/shard_map/em_step/pallas_call | solution.py:328
  31.4 0.0 copy-start
  31.4 1.5 %copy.14 = f32[480,32]{0,1:T(8,128)} copy(f32[480,32]{0,1:T(8,128)} %bitcast.9) | data formatting | bytes 122880
  33.0 1.5 %copy.15 = f32[480,32]{0,1:T(8,128)} copy(f32[480,32]{0,1:T(8,128)} %bitcast.8) | data formatting | bytes 122880
  34.4 0.0 copy-start.1
  34.4 1.3 %copy.16 = f32[32,128]{1,0:T(8,128)} copy(f32[32,128]{1,0:T(8,128)} %get-tuple-element.22) | data formatting | bytes 32768
  35.8 0.0 copy-done.1
  35.8 0.6 %copy.17 = f32[32,128]{1,0:T(8,128)} copy(f32[32,128]{1,0:T(8,128)S(1)} %copy-done.1) | data formatting | bytes 32768
  36.4 0.0 copy-done
  36.4 0.7 %copy.18 = f32[32,16,128]{2,1,0:T(8,128)} copy(f32[32,16,128]{2,1,0:T(8,128)S(1)} %bitcast.6) | data formatting | bytes 524288
Async XLA Ops:
  31.4 4.9 %copy-start = (f32[512,128]{1,0:T(8,128)S(1)}, f32[512,128]{1,0:T(8,128)}, u32[]{:S(2)}) copy-start(f32[512,128]{1,0:T(8,128)} %get-tuple-element.14) | copy-start | bytes 786436
  34.4 1.3 %copy-start.1 = (f32[32,128]{1,0:T(8,128)S(1)}, f32[32,128]{1,0:T(8,128)}, u32[]{:S(2)}) copy-start(f32[32,128]{1,0:T(8,128)} %get-tuple-element.23) | copy-start | bytes 49156

commit v2 on v1

--- a/solution.py
+++ b/solution.py
@@ -11,6 +11,8 @@
 MESH = pl.DeviceIdType.MESH
 F32 = jnp.float32
 BF16 = jnp.bfloat16
+LIMIT = 67043328 - 491520
+MOST = 5
 
 
 def normalize(fractions, gradient, second):
@@ -83,12 +85,12 @@
 
 def kernel(
     dims,
-    geno, counts, resid, freqs,
+    geno_in, counts_in, resid_in, freqs_in,
     q_out, g_out, p_out, pg_out, z_out,
-    dos, qf, gf, fcol, frow, ebuf, tbuf,
+    geno, counts, resid, freqs, dos, qf, gf, fcol, frow, ebuf, tbuf,
     acc_ex, acc_sc, acc_in,
     xs, xr, zs, zr, go, gp, fs, fr, ss, sr,
-    xs_s, xs_r, zs_s, zs_r, za_s, za_r, xa_s, xa_r, f_s, f_r, s_s, s_r,
+    xs_s, xs_r, zs_s, zs_r, za_s, za_r, xa_s, xa_r, f_s, f_r, s_s, s_r, in_s,
 ):
     chunks, width, half, zs_n, rows, variant_count, sample_count, share, var_n = dims
     anc = freqs.shape[0]
@@ -102,10 +104,26 @@
     twin = {"smp": 1 - core}
     z_peers = [{"var": lax.rem(z + d, zs_n) * 2 + x} for d in range(1, zs_n)]
 
+    def load(src, dst, which, base=None, size=None):
+        if base is not None:
+            src, dst = src.at[pl.ds(base, size), :], dst.at[pl.ds(base, size), :]
+        return pltpu.make_async_copy(src, dst, in_s.at[which])
+
+    far_half = pl.multiple_of((1 - x) * half, 128)
+    near_half = pl.multiple_of(x * half, 128)
+    freqs_load = load(freqs_in, freqs, 0)
+    counts_load = load(counts_in, counts, 1)
+    far_load = load(geno_in, geno, 2, far_half, half)
+    near_load = load(geno_in, geno, 3, near_half, half)
+    resid_load = load(resid_in, resid, 4)
+    for item in (freqs_load, counts_load, far_load, near_load, resid_load):
+        item.start()
+
     barrier = pltpu.get_barrier_semaphore()
     for peer in [partner, twin] + z_peers:
         pl.semaphore_signal(barrier, inc=1, device_id=peer, device_id_type=MESH)
 
+    freqs_load.wait()
     p = freqs[...]
     p_hi, p_lo = split(p)
     stack = jnp.concatenate([p_hi.astype(F32), p_lo.astype(F32)] * 2, axis=0)
@@ -198,14 +216,19 @@
     def x_gather(c):
         return copy(go.at[c], gp.at[c], xa_s.at[c], xa_r.at[c], partner)
 
+    counts_load.wait()
+    far_load.wait()
+    xs[0] = first_pass(lanes(1 - x, 0))
     pl.semaphore_wait(barrier, 2 + len(z_peers))
+    x_reduce(0).start()
 
     def step_far(c, carry):
         xs[c] = first_pass(lanes(1 - x, c))
         x_reduce(c).start()
         return carry
 
-    lax.fori_loop(0, chunks, step_far, 0)
+    lax.fori_loop(1, chunks, step_far, 0)
+    near_load.wait()
 
     def step_near(c, carry):
         g = first_pass(lanes(x, c))
@@ -236,6 +259,7 @@
 
     lax.fori_loop(0, chunks, step_sum, 0)
 
+    resid_load.wait()
     freq_copy.wait_recv()
     sums = fs[...] + fr[...]
     excess_sum = sums[0:anc, :]
@@ -291,6 +315,28 @@
         at = slice(traits * k, traits * (k + 1))
         z_out[at, :] = (ss[at, :] + sr[at, :]) * scale[k : k + 1, :]
     score_copy.wait_send()
+
+
+def store_kernel(*refs):
+    count = len(refs) // 2
+    sems = refs[-1]
+    copies = [pltpu.make_async_copy(refs[i], refs[count + i], sems.at[i]) for i in range(count)]
+    for item in copies:
+        item.start()
+    for item in copies:
+        item.wait()
+
+
+def store(*arrays):
+    return pl.pallas_call(
+        store_kernel,
+        out_shape=tuple(jax.ShapeDtypeStruct(a.shape, a.dtype) for a in arrays),
+        in_specs=[pl.BlockSpec(memory_space=pltpu.VMEM)] * len(arrays),
+        out_specs=(pl.BlockSpec(memory_space=pl.ANY),) * len(arrays),
+        scratch_shapes=[pltpu.SemaphoreType.DMA((len(arrays),))],
+        compiler_params=pltpu.CompilerParams(vmem_limit_bytes=1024 * 1024),
+        name="store",
+    )(*arrays)
 
 
 def fits(genotypes, residuals, freqs, var_n):
@@ -318,25 +364,29 @@
     rows = anc // zs_n
     half = samples // 2
     tiles = half // 128
-    chunks = max(n for n in range(1, 6) if tiles % n == 0)
+    chunks = max(n for n in range(1, MOST + 1) if tiles % n == 0)
     width = half // chunks
     share = samples // var_n
     dims = (chunks, width, half, zs_n, rows, mv * var_n, samples * lax.axis_size("smp"), share, var_n)
     vmem = pl.BlockSpec(memory_space=pltpu.VMEM)
     dma = pltpu.SemaphoreType.DMA
     part = pltpu.VMEM((chunks, anc, width), F32)
-    q_t, g_t, p_new, p_grad, z_flat = pl.pallas_call(
+    results = pl.pallas_call(
         functools.partial(kernel, dims),
         out_shape=(
-            jax.ShapeDtypeStruct((anc, share), F32),
-            jax.ShapeDtypeStruct((anc, share), F32),
-            jax.ShapeDtypeStruct((anc, mv), F32),
-            jax.ShapeDtypeStruct((anc, mv), F32),
-            jax.ShapeDtypeStruct((anc * traits, mv), F32),
+            pltpu.VMEM((anc, share), F32),
+            pltpu.VMEM((anc, share), F32),
+            pltpu.VMEM((anc, mv), F32),
+            pltpu.VMEM((anc, mv), F32),
+            pltpu.VMEM((anc * traits, mv), F32),
         ),
-        in_specs=[vmem] * 4,
+        in_specs=[pl.BlockSpec(memory_space=pltpu.HBM)] * 4,
         out_specs=(vmem,) * 5,
         scratch_shapes=[
+            pltpu.VMEM((samples, mv), BF16),
+            pltpu.VMEM((anc, samples), jnp.int32),
+            pltpu.VMEM((traits, samples), jnp.int32),
+            pltpu.VMEM((anc, mv), F32),
             pltpu.VMEM((mv, samples), BF16),
             pltpu.VMEM((anc, samples), F32),
             pltpu.VMEM((anc, samples), F32),
@@ -358,11 +408,12 @@
             dma((chunks, zs_n - 1)), dma((chunks, zs_n - 1)),
             dma((chunks, zs_n - 1)), dma((chunks, zs_n - 1)),
             dma((chunks,)), dma((chunks,)),
-            dma, dma, dma, dma,
+            dma, dma, dma, dma, dma((5,)),
         ],
-        compiler_params=pltpu.CompilerParams(collective_id=0, has_side_effects=True),
+        compiler_params=pltpu.CompilerParams(collective_id=0, has_side_effects=True, vmem_limit_bytes=LIMIT),
         name="em_step",
     )(genotypes, ancestry_counts.T, residuals.T, freqs)
+    q_t, g_t, p_new, p_grad, z_flat = store(*results)
     return (q_t.T, g_t.T, p_new, p_grad, z_flat.reshape(anc, traits, mv))
 
 

time: 37.4 us -> 29.9 us (0.80)
  local copies, waits for them, and re-layouts: 5.64 us -> 0 us
  Pallas kernels: 30.8 us -> 29.1 us
    unnamed x9 -> x0, local copies, waits for them, and re-layouts: 5.64 us -> none
    pallas_call x1 -> x2, Pallas kernels: 30.8 us -> 29.1 us  [the longest x1 28.3 us: shards(): pl.pallas_call(functools.partial(kernel, dims), out_shape=(pltpu.VMEM((an...]
where the time goes in v2:
time: 29.9 us; the launch traced here: 29.7 us
  Pallas kernels  29.1 us (97%)
  between operations  0.64 us (2%)
    pallas_call x1, Pallas kernels, shards(): pl.pallas_call(functools.partial(kernel, dims), out_shape=(pltpu.VMEM((an...  28.3 us
    pallas_call x1, Pallas kernels, store(): pl.pallas_call(store_kernel, out_shape=tuple((jax.ShapeDtypeStruct(a.shap...  0.8 us

profile of v2, /device:TPU:0, one launch (start us, length us, event | category | flops | bytes accessed | tf_op | source)
XLA Modules:
  0.0 29.7 jit_solution(1178097710724333093)
XLA Ops:
  0.6 28.3 %em_step.1 = (f32[32,480]{1,0:T(8,128)S(1)}, f32[32,480]{1,0:T(8,128)S(1)}, f32[32,128]{1,0:T(8,128)S(1)}, f32[32,128]{1,0:T(8,128)S(1)}, f32[512,128]{1,0:T(8,128)S(1)}) custom-call(bf16[3840,128]{1,0:T(8,128)(2,1)} %geno_in.1, s32[32,3840]{1,0:T(8,128)} %bitcast.5, s32[16,3840]{1,0:T(8,128)} %bitcast.6, f32[32,128]{1,0:T(8,128)} %freqs_in.1), custom_call_target="tpu_custom_call" | custom-call | tf_op jit(solution)/shard_map/em_step/pallas_call | solution.py:374
  28.9 0.8 %store.1 = (f32[32,480]{1,0:T(8,128)}, f32[32,480]{1,0:T(8,128)}, f32[32,128]{1,0:T(8,128)}, f32[32,128]{1,0:T(8,128)}, f32[512,128]{1,0:T(8,128)}) custom-call(f32[32,480]{1,0:T(8,128)S(1)} %get-tuple-element.15.refs_0_, f32[32,480]{1,0:T(8,128)S(1)} %get-tuple-element.16.refs_1_, f32[32,128]{1,0:T(8,128)S(1)} %get-tuple-element.17.refs_2_, ...), custom_call_target="tpu_custom_call" | custom-call | tf_op jit(solution)/shard_map/store/pallas_call | solution.py:331

commit v3 on v2

--- a/solution.py
+++ b/solution.py
@@ -213,8 +213,11 @@
         piece = go.at[c, pl.ds(source, rows), :]
         return copy(piece, piece, za_s.at[c, d - 1], za_r.at[c, d - 1], z_peers[d - 1])
 
-    def x_gather(c):
-        return copy(go.at[c], gp.at[c], xa_s.at[c], xa_r.at[c], partner)
+    def x_gather(c, d):
+        source = pl.multiple_of(lax.rem(z + zs_n - d, zs_n) * rows, 8)
+        return copy(
+            go.at[c, pl.ds(source, rows), :], gp.at[c, pl.ds(source, rows), :], xa_s.at[c, d], xa_r.at[c, d], partner
+        )
 
     counts_load.wait()
     far_load.wait()
@@ -255,6 +258,7 @@
         go[c, pl.ds(mine, rows), :] = total
         for d in range(1, zs_n):
             z_gather(c, d).start()
+        x_gather(c, 0).start()
         return carry
 
     lax.fori_loop(0, chunks, step_sum, 0)
@@ -271,14 +275,15 @@
     def step_own(c, carry):
         for d in range(1, zs_n):
             z_gathered(c, d).wait_recv()
-        x_gather(c).start()
+            x_gather(c, d).start()
         second_pass(lanes(x, c), go[c])
         return carry
 
     lax.fori_loop(0, chunks, step_own, 0)
 
     def step_other(c, carry):
-        x_gather(c).wait_recv()
+        for d in range(zs_n):
+            x_gather(c, d).wait_recv()
         second_pass(lanes(1 - x, c), gp[c])
         return carry
 
@@ -300,7 +305,8 @@
 
     def drain(c, carry):
         x_reduce(c).wait_send()
-        x_gather(c).wait_send()
+        for d in range(zs_n):
+            x_gather(c, d).wait_send()
         for d in range(1, zs_n):
             z_reduce(c, d).wait_send()
             z_gather(c, d).wait_send()
@@ -407,7 +413,7 @@
             dma((chunks,)), dma((chunks,)),
             dma((chunks, zs_n - 1)), dma((chunks, zs_n - 1)),
             dma((chunks, zs_n - 1)), dma((chunks, zs_n - 1)),
-            dma((chunks,)), dma((chunks,)),
+            dma((chunks, zs_n)), dma((chunks, zs_n)),
             dma, dma, dma, dma, dma((5,)),
         ],
         compiler_params=pltpu.CompilerParams(collective_id=0, has_side_effects=True, vmem_limit_bytes=LIMIT),

time: 29.9 us -> 30.2 us (1.010)
  no operation moved by 1% of the time
where the time goes in v3:
time: 30.2 us; the launch traced here: 30 us
  Pallas kernels  29.4 us (97%)
  between operations  0.64 us (2%)
    pallas_call x1, Pallas kernels, shards(): pl.pallas_call(functools.partial(kernel, dims), out_shape=(pltpu.VMEM((an...  28.6 us
    pallas_call x1, Pallas kernels, store(): pl.pallas_call(store_kernel, out_shape=tuple((jax.ShapeDtypeStruct(a.shap...  0.8 us

profile of v3, /device:TPU:0, one launch (start us, length us, event | category | flops | bytes accessed | tf_op | source)
XLA Modules:
  0.0 30.0 jit_solution(12637134367218992840)
XLA Ops:
  0.6 28.6 %em_step.1 = (f32[32,480]{1,0:T(8,128)S(1)}, f32[32,480]{1,0:T(8,128)S(1)}, f32[32,128]{1,0:T(8,128)S(1)}, f32[32,128]{1,0:T(8,128)S(1)}, f32[512,128]{1,0:T(8,128)S(1)}) custom-call(bf16[3840,128]{1,0:T(8,128)(2,1)} %geno_in.1, s32[32,3840]{1,0:T(8,128)} %bitcast.5, s32[16,3840]{1,0:T(8,128)} %bitcast.6, f32[32,128]{1,0:T(8,128)} %freqs_in.1), custom_call_target="tpu_custom_call" | custom-call | tf_op jit(solution)/shard_map/em_step/pallas_call | solution.py:380
  29.2 0.8 %store.1 = (f32[32,480]{1,0:T(8,128)}, f32[32,480]{1,0:T(8,128)}, f32[32,128]{1,0:T(8,128)}, f32[32,128]{1,0:T(8,128)}, f32[512,128]{1,0:T(8,128)}) custom-call(f32[32,480]{1,0:T(8,128)S(1)} %get-tuple-element.15.refs_0_, f32[32,480]{1,0:T(8,128)S(1)} %get-tuple-element.16.refs_1_, f32[32,128]{1,0:T(8,128)S(1)} %get-tuple-element.17.refs_2_, ...), custom_call_target="tpu_custom_call" | custom-call | tf_op jit(solution)/shard_map/store/pallas_call | solution.py:337
